TPU v7x, 32 devices: a whole 2x2x4 slice. The times are simulated.
32 devices in a mesh: freq: 4 (over z), trace: 8 (over y, x, core).
Axes of the slice: x: 2, y: 2, z: 4, core: 2. Of those that a mesh axis runs over, the one named last changes fastest.
Arguments:
- recorded: float32 [8, 2, 2048, 1024], P(None, None, 'freq', 'trace'), may hold values from -16 to 16
- multiples: float32 [8, 2, 2048, 1024], P(None, None, 'freq', 'trace'), may hold values from -6 to 6
Outputs:
- primaries: float32 [8, 2, 2048, 1024], P(None, None, 'freq', 'trace')
- filters: float32 [8, 2, 32, 64], P(None, None, 'freq')
All inputs are finite; a program needn't handle non-finite values.
Results may differ from a plain program's by a relative error of at most 0.0001.
Values sent between devices are 32-bit elements; how exact they have to be, the bound alone decides.
A program may use at most 128 MiB of HBM per device.

v0:
```python
import jax
import jax.numpy as jnp
from jax import lax
from jax.sharding import PartitionSpec as P

FB = 64
TAPS = 64
ITERS = 3


def with_halo(value, sides, width):
    for axis, dim in sides:
        size, length = (lax.axis_size(axis), value.shape[dim])
        up = [(i, (i + 1) % size) for i in range(size - 1)]
        down = [(j, i) for i, j in up]
        last = lax.slice_in_dim(value, length - width, length, axis=dim)
        first = lax.slice_in_dim(value, 0, width, axis=dim)
        before = lax.ppermute(last, axis, up)
        after = lax.ppermute(first, axis, down)
        value = jnp.concatenate([before, value, after], axis=dim)
    return value


def toeplitz_rows(taps_vec, trace_rows):
    tap_count = taps_vec.shape[-1]
    window_len = trace_rows + tap_count
    leading = taps_vec.shape[:-1]
    padded = jnp.concatenate(
        [
            jnp.zeros(leading + (1,), jnp.float32),
            taps_vec[..., ::-1],
            jnp.zeros(leading + (trace_rows,), jnp.float32),
        ],
        -1,
    )
    repeated = jnp.tile(padded, (1,) * len(leading) + (trace_rows,))
    return repeated[..., : trace_rows * window_len].reshape(leading + (trace_rows, window_len))


def product(left, right):
    return jnp.einsum("bfj,bxj->bfx", left, right, precision=lax.Precision.HIGHEST)


def correlate(left, right):
    return jnp.einsum("bfj,bfx->bxj", left, right, precision=lax.Precision.HIGHEST)


def forward_one(window, taps_vec):
    trace_rows = window.shape[-1] - taps_vec.shape[-1]
    toeplitz = toeplitz_rows(taps_vec, trace_rows)
    real_part = product(window[0], toeplitz[0]) - product(window[1], toeplitz[1])
    imag_part = product(window[0], toeplitz[1]) + product(window[1], toeplitz[0])
    return jnp.stack([real_part, imag_part])


def adjoint_one(window, residual, tap_count):
    real_part = correlate(window[0], residual[0]) + correlate(window[1], residual[1])
    imag_part = correlate(window[0], residual[1]) - correlate(window[1], residual[0])
    crossed = jnp.stack([real_part, imag_part])
    trace_rows, window_len = crossed.shape[-2:]
    leading = crossed.shape[:-2]
    flattened = crossed.reshape(leading + (trace_rows * window_len,))
    flattened = jnp.concatenate([flattened, jnp.zeros(leading + (trace_rows,), jnp.float32)], -1)
    column_sums = jnp.sum(flattened.reshape(leading + (trace_rows, window_len + 1)), axis=-2)
    return column_sums[..., 1 : tap_count + 1][..., ::-1]


def bending(edge_pad):
    return 2.0 * edge_pad[:, :, 1:-1] - edge_pad[:, :, :-2] - edge_pad[:, :, 2:]


def inner_sum(left, right):
    return jnp.sum(left * right, axis=(1, 2, 3))


def body(recorded, multiples):
    half_taps = TAPS // 2
    trace_rows = multiples.shape[3]
    edged = with_halo(multiples, (("trace", 3),), half_taps)
    shot_count, part_count, freq_rows, window_len = edged.shape
    block_count = freq_rows // FB
    windows = edged.reshape(shot_count, part_count, block_count, FB, window_len)
    trace_count = lax.axis_size("trace")
    weight = 0.5 * FB * trace_rows * trace_count
    residual = recorded
    shaping = jnp.zeros((shot_count, part_count, block_count, TAPS), jnp.float32)
    bent_sum = jnp.zeros_like(shaping)
    direction = shaping
    norm_now = jnp.ones((shot_count,), jnp.float32)
    for iteration in range(ITERS):
        pieces = residual.reshape(shot_count, part_count, block_count, FB, trace_rows)
        gradient = (
            lax.psum(
                lax.map(lambda paired: adjoint_one(paired[0], paired[1], TAPS), (windows, pieces)),
                "trace",
            )
            - bent_sum
        )
        norm_next = lax.psum(inner_sum(gradient, gradient), "freq")
        if iteration == 0:
            direction = gradient
        else:
            direction = gradient + (norm_next / norm_now)[:, None, None, None] * direction
        norm_now = norm_next
        result = lax.map(lambda paired: forward_one(paired[0], paired[1]), (windows, direction))
        applied = result.reshape(shot_count, part_count, freq_rows, trace_rows)
        edge_pad = with_halo(direction, (("freq", 2),), 1)
        smooth = weight * bending(edge_pad)
        energy_sum, smooth_sum = lax.psum(
            (jnp.sum(applied * applied, axis=(1, 2, 3)), inner_sum(direction, smooth)),
            ("freq", "trace"),
        )
        energy = energy_sum + smooth_sum / trace_count
        step_len = (norm_now / energy)[:, None, None, None]
        shaping = shaping + step_len * direction
        residual = residual - step_len * applied
        bent_sum = bent_sum + step_len * smooth
    return (residual, shaping)


def solution(mesh):
    return jax.shard_map(
        body,
        mesh=mesh,
        in_specs=(P(None, None, "freq", "trace"), P(None, None, "freq", "trace")),
        out_specs=(P(None, None, "freq", "trace"), P(None, None, "freq", None)),
        check_vma=False,
    )
```

profile of v0, /device:TPU:0, one launch (start us, length us, event | category | flops | bytes accessed | tf_op | source)
XLA Modules:
  0.0 1106.0 jit_solution(16259001931993445002)
XLA Ops:
  0.6 8.0 fusion.60
  27.1 8.8 pad_maximum_fusion
  35.8 140.7 %while.60 = (s32[]{:T(128)}, f32[8,2,8,64]{3,2,1,0:T(8,128)S(1)}, f32[8,2,8,64,128]{4,3,2,1,0:T(8,128)}, f32[8,2,8,64,192]{4,3,2,1,0:T(8,128)}, s32[]{:T(128)}, /*index=5*/s32[]{:T(128)}, s32[]{}, f32[]{:T(128)}) while((s32[]{:T(128)}, f32[8,2,8,64]{3,2,1,0:T(8,128)S(1)}, f32[8,2,8,64,128]{4,3,2,1,0:T(8,128)}, ...), condition=%wide.region_2.3_spmd, body=%wide.region_0.2_spmd.sunk | while | flops 606346240 | bytes 22103216 | solution.py:94
  84.0 4.2 reshape.130
  101.6 4.2 reshape.130
  136.8 4.2 reshape.130
  176.5 40.3 %psum.84 = f32[8,2,8,64]{3,2,1,0:T(8,128)S(1)} all-reduce(f32[8,2,8,64]{3,2,1,0:T(8,128)S(1)} %get-tuple-element.134), channel_id=1, replica_groups=mesh['freq'=4,'trace'=8] {'trace'}, use_global_device_ids=true, to_apply=%region_3.4 | all-reduce | flops 8192 | bytes 65536 | tf_op jit(solution)/shard_map/psum | solution.py:93
  224.4 120.3 %while.61 = (s32[]{:T(128)}, f32[8,2,8,64,128]{4,3,2,1,0:T(8,128)}, f32[8,2,8,64,192]{4,3,2,1,0:T(8,128)}, f32[8,2,8,64]{3,2,1,0:T(8,128)S(1)}, s32[]{:T(128)}, /*index=5*/f32[]{:T(128)}, f32[]{:T(128)}, s32[]{:T(128)}, s32[]{}) while((s32[]{:T(128)}, f32[8,2,8,64,128]{4,3,2,1,0:T(8,128)}, f32[8,2,8,64,192]{4,3,2,1,0:T(8,128)}, ...), condition=%wide.region_7.8_spmd, body=%wide.region_6.7_spmd.sunk | while | flops 604248064 | bytes 18950932 | solution.py:105
  347.5 13.0 %psum.85 = f32[8]{0:T(128)S(1)} all-reduce(f32[8]{0:T(128)S(1)} %get-tuple-element.141), channel_id=1, replica_groups=mesh['freq'=4,'trace'=8] {'freq'}, use_global_device_ids=true, to_apply=%region_5.6 | all-reduce | flops 8 | bytes 64 | tf_op jit(solution)/shard_map/psum | solution.py:99
  360.5 37.8 %all-reduce.5 = (f32[8]{0:T(128)S(1)}, f32[8]{0:T(128)S(1)}) all-reduce(f32[8]{0:T(128)S(1)} %multiply_reduce_fusion.2, f32[8]{0:T(128)S(1)} %get-tuple-element.140), channel_id=1, replica_groups=mesh['freq'=4,'trace'=8] {'freq','trace'}, use_global_device_ids=true, to_apply=%region_9.10 | all-reduce | flops 16 | bytes 128 | tf_op jit(solution)/shard_map/psum | solution.py:109
  398.3 6.0 fusion.47
  404.3 140.6 %while.62 = (s32[]{:T(128)}, f32[8,2,8,64]{3,2,1,0:T(8,128)S(1)}, f32[8,2,8,64,128]{4,3,2,1,0:T(8,128)}, f32[8,2,8,64,192]{4,3,2,1,0:T(8,128)}, s32[]{:T(128)}, /*index=5*/s32[]{:T(128)}, s32[]{}, f32[]{:T(128)}) while((s32[]{:T(128)}, f32[8,2,8,64]{3,2,1,0:T(8,128)S(1)}, f32[8,2,8,64,128]{4,3,2,1,0:T(8,128)}, ...), condition=%wide.region_14.15_spmd, body=%wide.region_12.14_spmd.sunk | while | flops 606346240 | bytes 22103216 | solution.py:94
  417.3 4.2 reshape.131
  434.9 4.2 reshape.131
  470.0 4.2 reshape.131
  487.6 4.2 reshape.131
  522.8 4.2 reshape.131
  544.9 23.8 %psum.88 = f32[8,2,8,64]{3,2,1,0:T(8,128)S(1)} all-reduce(f32[8,2,8,64]{3,2,1,0:T(8,128)S(1)} %get-tuple-element.136), channel_id=1, replica_groups=mesh['freq'=4,'trace'=8] {'trace'}, use_global_device_ids=true, to_apply=%region_15.16 | all-reduce | flops 8192 | bytes 65536 | tf_op jit(solution)/shard_map/psum | solution.py:93
  569.0 11.2 %psum.89 = f32[8]{0:T(128)S(1)} all-reduce(f32[8]{0:T(128)S(1)} %multiply_reduce_fusion.5), channel_id=1, replica_groups=mesh['freq'=4,'trace'=8] {'freq'}, use_global_device_ids=true, to_apply=%region_17.18 | all-reduce | flops 8 | bytes 64 | tf_op jit(solution)/shard_map/psum | solution.py:99
  585.9 120.0 %while.63 = (s32[]{:T(128)}, f32[8,2,8,64,128]{4,3,2,1,0:T(8,128)}, f32[8,2,8,64,192]{4,3,2,1,0:T(8,128)}, f32[8,2,8,64]{3,2,1,0:T(8,128)S(1)}, s32[]{:T(128)}, /*index=5*/f32[]{:T(128)}, f32[]{:T(128)}, s32[]{:T(128)}, s32[]{}) while((s32[]{:T(128)}, f32[8,2,8,64,128]{4,3,2,1,0:T(8,128)}, f32[8,2,8,64,192]{4,3,2,1,0:T(8,128)}, ...), condition=%wide.region_19.20_spmd, body=%wide.region_18.19_spmd.sunk | while | flops 604248064 | bytes 18950932 | solution.py:105
  708.8 40.5 %all-reduce.4 = (f32[8]{0:T(128)S(1)}, f32[8]{0:T(128)S(1)}) all-reduce(f32[8]{0:T(128)S(1)} %multiply_reduce_fusion.1, f32[8]{0:T(128)S(1)} %multiply_reduce_fusion.4), channel_id=1, replica_groups=mesh['freq'=4,'trace'=8] {'freq','trace'}, use_global_device_ids=true, to_apply=%region_21.22 | all-reduce | flops 16 | bytes 128 | tf_op jit(solution)/shard_map/psum | solution.py:109
  749.3 6.0 fusion.46
  755.3 140.6 %while.64 = (s32[]{:T(128)}, f32[8,2,8,64]{3,2,1,0:T(8,128)S(1)}, f32[8,2,8,64,128]{4,3,2,1,0:T(8,128)}, f32[8,2,8,64,192]{4,3,2,1,0:T(8,128)}, s32[]{:T(128)}, /*index=5*/s32[]{:T(128)}, s32[]{}, f32[]{:T(128)}) while((s32[]{:T(128)}, f32[8,2,8,64]{3,2,1,0:T(8,128)S(1)}, f32[8,2,8,64,128]{4,3,2,1,0:T(8,128)}, ...), condition=%wide.region_26.27_spmd, body=%wide.region_24.26_spmd.sunk | while | flops 606346240 | bytes 22103216 | solution.py:94
  768.3 4.2 reshape.132
  785.9 4.2 reshape.132
  821.1 4.2 reshape.132
  838.6 4.2 reshape.132
  896.0 23.5 %psum.92 = f32[8,2,8,64]{3,2,1,0:T(8,128)S(1)} all-reduce(f32[8,2,8,64]{3,2,1,0:T(8,128)S(1)} %get-tuple-element.138), channel_id=1, replica_groups=mesh['freq'=4,'trace'=8] {'trace'}, use_global_device_ids=true, to_apply=%region_27.28 | all-reduce | flops 8192 | bytes 65536 | tf_op jit(solution)/shard_map/psum | solution.py:93
  919.7 9.9 psum.93
  936.1 119.7 %while.65 = (s32[]{:T(128)}, f32[8,2,8,64,128]{4,3,2,1,0:T(8,128)}, f32[8,2,8,64,192]{4,3,2,1,0:T(8,128)}, f32[8,2,8,64]{3,2,1,0:T(8,128)S(1)}, s32[]{:T(128)}, /*index=5*/f32[]{:T(128)}, f32[]{:T(128)}, s32[]{:T(128)}, s32[]{}) while((s32[]{:T(128)}, f32[8,2,8,64,128]{4,3,2,1,0:T(8,128)}, f32[8,2,8,64,192]{4,3,2,1,0:T(8,128)}, ...), condition=%wide.region_31.32_spmd, body=%wide.region_30.31_spmd.sunk | while | flops 604248064 | bytes 18950932 | solution.py:105
  1058.7 40.3 %all-reduce.3 = (f32[8]{0:T(128)S(1)}, f32[8]{0:T(128)S(1)}) all-reduce(f32[8]{0:T(128)S(1)} %multiply_reduce_fusion, f32[8]{0:T(128)S(1)} %fusion.51), channel_id=1, replica_groups=mesh['freq'=4,'trace'=8] {'freq','trace'}, use_global_device_ids=true, to_apply=%region_33.34 | all-reduce | flops 16 | bytes 128 | tf_op jit(solution)/shard_map/psum | solution.py:109
  1099.7 6.1 fusion.45
  (753 shorter events, 775.5 us)
Async XLA Ops:
  11.4 6.8 collective-permute-start
  16.7 6.7 collective-permute-start.1
  216.9 130.4 %collective-permute-start.2 = (f32[8,2,1,64]{3,2,1,0:T(1,128)S(1)}, f32[8,2,1,64]{3,2,1,0:T(1,128)S(1)}, u32[]{:S(2)}, u32[]{:S(2)}) collective-permute-start(f32[8,2,1,64]{3,2,1,0:T(1,128)S(1)} %get-tuple-element.214), channel_id=1, source_target_pairs={{0,8},{8,16},{16,24},{1,9},{9,17},{17,25},{2,10},{10,18},{18,26},{... | collective-permute-start | bytes 12296 | tf_op jit(solution)/shard_map/ppermute | solution.py:18
  220.3 126.9 %collective-permute-start.3 = (f32[8,2,1,64]{3,2,1,0:T(1,128)S(1)}, f32[8,2,1,64]{3,2,1,0:T(1,128)S(1)}, u32[]{:S(2)}, u32[]{:S(2)}) collective-permute-start(f32[8,2,1,64]{3,2,1,0:T(1,128)S(1)} %get-tuple-element.215), channel_id=1, source_target_pairs={{8,0},{16,8},{24,16},{9,1},{17,9},{25,17},{10,2},{18,10},{26,18},{... | collective-permute-start | bytes 12296 | tf_op jit(solution)/shard_map/ppermute | solution.py:19
  580.3 128.3 %collective-permute-start.4 = (f32[8,2,1,64]{3,2,1,0:T(1,128)S(1)}, f32[8,2,1,64]{3,2,1,0:T(1,128)S(1)}, u32[]{:S(2)}, u32[]{:S(2)}) collective-permute-start(f32[8,2,1,64]{3,2,1,0:T(1,128)S(1)} %get-tuple-element.212), channel_id=1, source_target_pairs={{0,8},{8,16},{16,24},{1,9},{9,17},{17,25},{2,10},{10,18},{18,26},{... | collective-permute-start | bytes 12296 | tf_op jit(solution)/shard_map/ppermute | solution.py:18
  581.9 126.7 %collective-permute-start.5 = (f32[8,2,1,64]{3,2,1,0:T(1,128)S(1)}, f32[8,2,1,64]{3,2,1,0:T(1,128)S(1)}, u32[]{:S(2)}, u32[]{:S(2)}) collective-permute-start(f32[8,2,1,64]{3,2,1,0:T(1,128)S(1)} %get-tuple-element.213), channel_id=1, source_target_pairs={{8,0},{16,8},{24,16},{9,1},{17,9},{25,17},{10,2},{18,10},{26,18},{... | collective-permute-start | bytes 12296 | tf_op jit(solution)/shard_map/ppermute | solution.py:19
  929.8 128.7 %collective-permute-start.6 = (f32[8,2,1,64]{3,2,1,0:T(1,128)S(1)}, f32[8,2,1,64]{3,2,1,0:T(1,128)S(1)}, u32[]{:S(2)}, u32[]{:S(2)}) collective-permute-start(f32[8,2,1,64]{3,2,1,0:T(1,128)S(1)} %get-tuple-element.210), channel_id=1, source_target_pairs={{0,8},{8,16},{16,24},{1,9},{9,17},{17,25},{2,10},{10,18},{18,26},{... | collective-permute-start | bytes 12296 | tf_op jit(solution)/shard_map/ppermute | solution.py:18
  932.1 126.4 %collective-permute-start.7 = (f32[8,2,1,64]{3,2,1,0:T(1,128)S(1)}, f32[8,2,1,64]{3,2,1,0:T(1,128)S(1)}, u32[]{:S(2)}, u32[]{:S(2)}) collective-permute-start(f32[8,2,1,64]{3,2,1,0:T(1,128)S(1)} %get-tuple-element.211), channel_id=1, source_target_pairs={{8,0},{16,8},{24,16},{9,1},{17,9},{25,17},{10,2},{18,10},{26,18},{... | collective-permute-start | bytes 12296 | tf_op jit(solution)/shard_map/ppermute | solution.py:19
where the time goes:
time: 1120 us; the launch traced here: 1110 us
  matrix products  463 us (41%)
  local copies, waits for them, and re-layouts  287 us (26%)
  blocking collectives  240 us (21%)
  other arithmetic  93.1 us (8%)
  starting transfers between devices  15.8 us (1%)
    dot_general x96, matrix products, correlate(): jnp.einsum('bfj,bfx->bxj', left, right, precision=lax.Precision.HIGHEST)  246 us
    dot_general x96, matrix products, product(): jnp.einsum('bfj,bxj->bfx', left, right, precision=lax.Precision.HIGHEST)  217 us
    psum x3, blocking collectives, body(): lax.psum((jnp.sum(applied * applied, axis=(1, 2, 3)), inner_sum(direction...  119 us
    reshape x24, local copies, waits for them, and re-layouts, adjoint_one(): flattened.reshape(leading + (trace_rows, window_len + 1))  102 us
    psum x3, blocking collectives, body(): lax.psum(lax.map(lambda paired: adjoint_one(paired[0], paired[1], TAPS),...  87.7 us
    another operation x48, local copies, waits for them, and re-layouts, toeplitz_rows(): repeated = jnp.tile(padded, (1,) * len(leading) + (trace_rows,))  57.1 us
    slice x24, local copies, waits for them, and re-layouts, forward_one(): toeplitz[0]  35.3 us
    psum x3, blocking collectives, body(): norm_next = lax.psum(inner_sum(gradient, gradient), 'freq')  34.1 us
  transfers between devices with their start and end apart: 8, of which 1 were waited for; matrix products, arithmetic and copies ran while one was open for 34% of the time, Pallas kernels for 0%

commit v1 on v0

v1 whole, which is shorter than its diff:
```python
import functools

import jax
import jax.numpy as jnp
from jax import lax
from jax.experimental import pallas as pl
from jax.experimental.pallas import tpu as pltpu
from jax.sharding import PartitionSpec as P

FB = 64
TAPS = 64
ITERS = 3
HALF = TAPS // 2
LANES = 128
ROWS = 4 + HALF
F32 = jnp.float32
BF16 = jnp.bfloat16


def lanes_of(shape):
    return lax.broadcasted_iota(jnp.int32, shape, len(shape) - 1)


def turn(value, shift):
    shift = shift % LANES
    return value if shift == 0 else pltpu.roll(value, shift, 1)


def split(value):
    high = value.astype(BF16)
    return high, (value - high.astype(F32)).astype(BF16)


def tiles(m_ref, left_ref, right_ref, b, part):
    group_rows = left_ref.shape[2]
    group, first = (b * FB) // group_rows, (b * FB) % group_rows
    main = m_ref[0, part, b * FB : (b + 1) * FB, :]
    left = turn(left_ref[0, part, first : first + FB, :], LANES - HALF - HALF * group)
    right = turn(right_ref[0, part, first : first + FB, :], -HALF * group)
    lane = lanes_of(main.shape)
    halo = jnp.where(lane < HALF, right, jnp.where(lane >= LANES - HALF, left, 0.0))
    return main, halo


def three(pair):
    (rh, rl), (ih, il) = pair
    return jnp.concatenate([rh, ih, rh, ih, rl, il], 0)


def three_re(pair):
    (rh, rl), (ih, il) = pair
    return jnp.concatenate([rh, ih, rl, il, rh, ih], 0)


def three_im(pair):
    (rh, rl), (ih, il) = pair
    return jnp.concatenate([ih, -rh, il, -rl, ih, -rh], 0)


def over_first(left, right):
    return lax.dot_general(left, right, (((0,), (0,)), ((), ())), preferred_element_type=F32)


def diagonals(main, halo, offset):
    lane = lanes_of((8, LANES))
    total = jnp.zeros((8, LANES), F32)
    for g in range(LANES // 8):
        shift = offset - 8 * g
        own = turn(main[8 * g : 8 * g + 8], shift)
        other = turn(halo[8 * g : 8 * g + 8], shift)
        outside = lane < shift if shift >= 0 else lane >= LANES + shift
        total = total + jnp.where(outside, other, own)
    row = lax.broadcasted_iota(jnp.int32, (8, LANES), 0)
    result = jnp.where(row == 0, total, 0.0)
    for s in range(1, 8):
        result = result + jnp.where(row == s, turn(total, -s), 0.0)
    return jnp.sum(result, axis=0, keepdims=True)


def stats_kernel(mask_ref, m_ref, left_ref, right_ref, rec_ref, out_ref):
    for b in range(m_ref.shape[2] // FB):
        windows, starts, ends, records = [], [], [], []
        for part in range(2):
            main, halo = tiles(m_ref, left_ref, right_ref, b, part)
            turned = turn(main, HALF)
            shifted = jnp.where(lanes_of(main.shape) < HALF, turn(halo, HALF), turned)
            windows.append(split(jnp.concatenate([main, halo], 1)))
            starts.append(split(jnp.concatenate([shifted, rec_ref[0, part, b * FB : (b + 1) * FB, :]], 1)))
            ends.append(split(turned))
        crossed = over_first(three(starts), jnp.concatenate([three_re(windows), three_im(windows)], 1))
        edge = over_first(three(ends)[:, :TAPS], jnp.concatenate([three_re(ends), three_im(ends)], 1))
        quads = []
        for first, offset in ((0, HALF), (LANES, HALF - 1)):
            for column in (0, 2 * LANES):
                rows = slice(first, first + LANES)
                quads.append(
                    diagonals(
                        crossed[rows, column : column + LANES],
                        crossed[rows, column + LANES : column + 2 * LANES],
                        offset,
                    )
                )
        quads[3] = -quads[3]
        real, imag = edge[:, :LANES], turn(edge[:, LANES:], TAPS)
        lane = lanes_of((HALF, LANES))
        corner = jnp.where(
            lane < HALF,
            real[:HALF],
            jnp.where(lane < TAPS, real[HALF:], jnp.where(lane < TAPS + HALF, imag[:HALF], imag[HALF:])),
        )
        corner = jnp.where(mask_ref[...] > 0.0, corner, 0.0)
        out_ref[0, :, b, :] = jnp.concatenate(quads + [corner], 0)


def exact(left, right):
    return jnp.dot(left, right, precision=lax.Precision.HIGHEST, preferred_element_type=F32)


def mirror(total):
    rows = lax.broadcasted_iota(jnp.int32, (LANES, LANES), 0)
    return (rows + lanes_of((LANES, LANES)) == total).astype(F32)


def total_of(value):
    return jnp.sum(jnp.sum(value, axis=1, keepdims=True), axis=0, keepdims=True)


def solve_kernel(weight, st_ref, out_ref, matrix):
    blocks = st_ref.shape[0] * st_ref.shape[3]

    def row(r):
        return st_ref[:, 0, r, :, :].reshape(blocks, LANES)

    lane = lanes_of((blocks, LANES))
    place = lane % TAPS
    is_real = lane < TAPS
    carry_right = place < HALF - 1
    carry_left = place > HALF
    in_right = place < HALF
    right = [None] * HALF
    for i in reversed(range(HALF)):
        value = jnp.where(in_right, row(4 + i), 0.0)
        if i + 1 < HALF:
            value = value + jnp.where(carry_right, turn(right[i + 1], -1), 0.0)
        right[i] = value
        if i >= 1:
            matrix[i - 1] = jnp.where(carry_right, turn(value, -1), 0.0)
    matrix[HALF - 1] = jnp.zeros((blocks, LANES), F32)
    last = None
    for i in range(HALF):
        value = jnp.where(in_right, 0.0, row(4 + i))
        if i:
            value = value + jnp.where(carry_left, turn(last, 1), 0.0)
        last = value
        matrix[HALF + i] = value
    lag_real = jnp.where(is_real, row(0), 0.0) + jnp.where(lane < HALF, right[0], 0.0)
    lag_imag = jnp.where(is_real, row(1), 0.0) + jnp.where(lane < HALF, turn(right[0], TAPS), 0.0)
    back = mirror(LANES)
    toep_real = jnp.where(is_real, lag_real, exact(lag_real, back))
    toep_imag = jnp.where(is_real, -lag_imag, exact(lag_imag, back))
    for t in range(TAPS):
        toep = jnp.where(is_real, turn(toep_real, t), turn(toep_imag, TAPS + t))
        matrix[t] = toep - jnp.where(is_real, matrix[t], -matrix[t])

    gradient = jnp.where(is_real, row(2), turn(row(3), TAPS))
    filters = jnp.zeros((blocks, LANES), F32)
    direction = norm_now = None
    none = jnp.zeros((1, LANES), F32)
    for iteration in range(ITERS):
        norm_next = total_of(gradient * gradient)
        if iteration == 0:
            direction = gradient
        else:
            direction = gradient + (norm_next / norm_now) * direction
        norm_now = norm_next
        by_real = jnp.zeros((blocks, LANES), F32)
        by_imag = jnp.zeros((blocks, LANES), F32)
        for t in range(TAPS):
            by_real = by_real + direction[:, t : t + 1] * matrix[t]
            by_imag = by_imag + direction[:, TAPS + t : TAPS + t + 1] * matrix[t]
        by_imag = turn(by_imag, TAPS)
        normal = by_real + jnp.where(is_real, -by_imag, by_imag)
        before = jnp.concatenate([none, direction[:-1]], 0)
        after = jnp.concatenate([direction[1:], none], 0)
        normal = normal + weight * (2.0 * direction - before - after)
        step_len = norm_now / total_of(direction * normal)
        filters = filters + step_len * direction
        gradient = gradient - step_len * normal
    out_ref[0, 0] = exact(filters, mirror(TAPS - 1))
    out_ref[0, 1] = exact(jnp.where(is_real, 0.0, filters), mirror(2 * TAPS - 1))


def forward_kernel(h_ref, m_ref, left_ref, right_ref, rec_ref, out_ref):
    rows = lax.broadcasted_iota(jnp.int32, (LANES, LANES), 0)
    tap = lanes_of((LANES, LANES)) + HALF - rows
    direct = (tap >= 0) & (tap < TAPS)
    for b in range(m_ref.shape[2] // FB):
        windows, bands = [], []
        for part in range(2):
            windows.append(split(jnp.concatenate(tiles(m_ref, left_ref, right_ref, b, part), 1)))
            base = jnp.where(lanes_of((1, LANES)) < TAPS, h_ref[0, part, b : b + 1, :], 0.0)
            base = pltpu.roll(jnp.broadcast_to(base, (8, LANES)), 0, 1, stride=1, stride_axis=0)
            ring = jnp.concatenate([turn(base, 8 * g - HALF) for g in range(LANES // 8)], 0)
            band = jnp.concatenate([jnp.where(direct, ring, 0.0), jnp.where(direct, 0.0, ring)], 0)
            bands.append(split(band))
        (rh, rl), (ih, il) = windows
        high, low = jnp.concatenate([rh, ih], 1), jnp.concatenate([rl, il], 1)
        sides = []
        for term in range(2):
            real, imag = bands[0][term], bands[1][term]
            sides.append(
                jnp.concatenate(
                    [jnp.concatenate([real, imag], 1), jnp.concatenate([-imag, real], 1)], 0
                )
            )
        both = jnp.dot(jnp.concatenate([high, low], 0), sides[0], preferred_element_type=F32)
        applied = both[:FB] + both[FB:] + jnp.dot(high, sides[1], preferred_element_type=F32)
        span = slice(b * FB, (b + 1) * FB)
        out_ref[0, 0, span, :] = rec_ref[0, 0, span, :] - applied[:, :LANES]
        out_ref[0, 1, span, :] = rec_ref[0, 1, span, :] - applied[:, LANES:]


def packed(value):
    count = LANES // HALF
    return jnp.concatenate(jnp.split(value, count, axis=2), axis=3)


def body(recorded, multiples):
    shots, parts, freq_rows, trace_rows = multiples.shape
    blocks = freq_rows // FB
    trace_count, freq_count = lax.axis_size("trace"), lax.axis_size("freq")
    me = lax.axis_index("trace")
    up = [(i, i + 1) for i in range(trace_count - 1)]
    down = [(j, i) for i, j in up]
    left = lax.ppermute(packed(multiples[..., trace_rows - HALF :]), "trace", up)
    right = lax.ppermute(packed(multiples[..., :HALF]), "trace", down)

    place = jnp.arange(LANES)[None, :] % TAPS < HALF
    mask = jnp.where(place, me == trace_count - 1, me == 0).astype(F32)

    field = pl.BlockSpec((1, parts, freq_rows, trace_rows), lambda s: (s, 0, 0, 0))
    side = pl.BlockSpec((1, parts) + left.shape[2:], lambda s: (s, 0, 0, 0))
    stats = pl.pallas_call(
        stats_kernel,
        grid=(shots,),
        in_specs=[pl.BlockSpec((1, LANES), lambda s: (0, 0)), field, side, side, field],
        out_specs=pl.BlockSpec((1, ROWS, blocks, LANES), lambda s: (s, 0, 0, 0)),
        out_shape=jax.ShapeDtypeStruct((shots, ROWS, blocks, LANES), F32),
        name="stats",
    )(mask, multiples, left, right, recorded)

    per_device = -(-shots // trace_count)
    extra = per_device * trace_count - shots
    if extra:
        stats = jnp.pad(stats, ((0, extra), (0, 0), (0, 0), (0, 0)))
    stats = lax.psum_scatter(stats, "trace", scatter_dimension=0, tiled=True)
    stats = lax.all_gather(stats, "freq", axis=0)

    weight = 0.5 * FB * trace_rows * trace_count
    all_blocks = blocks * freq_count
    solved = pl.pallas_call(
        functools.partial(solve_kernel, weight),
        grid=(per_device,),
        in_specs=[pl.BlockSpec((freq_count, 1, ROWS, blocks, LANES), lambda s: (0, s, 0, 0, 0))],
        out_specs=pl.BlockSpec((1, parts, all_blocks, LANES), lambda s: (s, 0, 0, 0)),
        out_shape=jax.ShapeDtypeStruct((per_device, parts, all_blocks, LANES), F32),
        scratch_shapes=[pltpu.VMEM((TAPS, all_blocks, LANES), F32)],
        name="solve",
    )(stats)
    mine = lax.dynamic_slice_in_dim(solved, lax.axis_index("freq") * blocks, blocks, axis=2)
    taps = lax.all_gather(mine, "trace", axis=0, tiled=True)[:shots]

    primaries = pl.pallas_call(
        forward_kernel,
        grid=(shots,),
        in_specs=[pl.BlockSpec((1, parts, blocks, LANES), lambda s: (s, 0, 0, 0)), field, side, side, field],
        out_specs=field,
        out_shape=jax.ShapeDtypeStruct(recorded.shape, F32),
        name="forward",
    )(taps, multiples, left, right, recorded)
    return primaries, taps[..., :TAPS]


def solution(mesh):
    spec = P(None, None, "freq", "trace")
    return jax.shard_map(
        body,
        mesh=mesh,
        in_specs=(spec, spec),
        out_specs=(spec, P(None, None, "freq", None)),
        check_vma=False,
    )
```

time: 1120 us -> 186 us (0.17); the launches traced: 1110 us -> 185 us
  matrix products: 463 us -> 0 us
  local copies, waits for them, and re-layouts: 287 us -> 7.28 us
  blocking collectives: 240 us -> 28.9 us
  other arithmetic: 93.1 us -> 3.25 us
  Pallas kernels: 0 us -> 67 us
  waiting for transfers between devices: 2.57 us -> 60.1 us
  between operations: 1.06 us -> 14.1 us
  starting transfers between devices: 15.8 us -> 4.41 us
    dot_general x192 -> x0, matrix products: 463 us -> none  [the longest x96 246 us: correlate(): jnp.einsum('bfj,bfx->bxj', left, right, precision=lax.Precision.HIGHEST)]
    psum x9 -> x0, blocking collectives: 240 us -> none  [the longest x3 119 us: body(): lax.psum((jnp.sum(applied * applied, axis=(1, 2, 3)), inner_sum(direction...]
    reshape x24 -> x0, local copies, waits for them, and re-layouts: 102 us -> none  [adjoint_one(): flattened.reshape(leading + (trace_rows, window_len + 1))]
    another operation x126 -> x0, local copies, waits for them, and re-layouts: 83.8 us -> none  [the longest x48 57.1 us: toeplitz_rows(): repeated = jnp.tile(padded, (1,) * len(leading) + (trace_rows,))]
    pallas_call x0 -> x3, Pallas kernels: none -> 67 us  [the longest x1 46.6 us: body(): pl.pallas_call(stats_kernel, grid=(shots,), in_specs=[pl.BlockSpec((1, LA...]
    reduce_scatter x0 -> x1, waiting for transfers between devices: none -> 58.2 us  [body(): stats = lax.psum_scatter(stats, 'trace', scatter_dimension=0, tiled=True)]
    slice x52 -> x0, local copies, waits for them, and re-layouts: 45.1 us -> none  [the longest x24 35.3 us: forward_one(): toeplitz[0]]
    another operation x24 -> x0, other arithmetic: 30 us -> none  [adjoint_one(): crossed = jnp.stack([real_part, imag_part])]
  transfers between devices with their start and end apart: 8 -> 3, of which waited for: 1 -> 2; matrix products, arithmetic and copies ran while one was open for 34% -> 1% of each run, Pallas kernels for 0% -> 0%
where the time goes in v1:
time: 186 us; the launch traced here: 185 us
  Pallas kernels  67 us (36%)
  waiting for transfers between devices  60.1 us (32%)
  blocking collectives  28.9 us (16%)
  between operations  14.1 us (8%)
  local copies, waits for them, and re-layouts  7.28 us (4%)
  starting transfers between devices  4.41 us (2%)
  other arithmetic  3.25 us (2%)
    reduce_scatter x1, waiting for transfers between devices, body(): stats = lax.psum_scatter(stats, 'trace', scatter_dimension=0, tiled=True)  58.2 us
    pallas_call x1, Pallas kernels, body(): pl.pallas_call(stats_kernel, grid=(shots,), in_specs=[pl.BlockSpec((1, LA...  46.6 us
    all_gather x1, blocking collectives, body(): stats = lax.all_gather(stats, 'freq', axis=0)  18.7 us
    pallas_call x1, Pallas kernels, body(): pl.pallas_call(forward_kernel, grid=(shots,), in_specs=[pl.BlockSpec((1,...  13 us
    all_gather x1, blocking collectives, body(): taps = lax.all_gather(mine, 'trace', axis=0, tiled=True)[:shots]  10.2 us
    pallas_call x1, Pallas kernels, body(): pl.pallas_call(functools.partial(solve_kernel, weight), grid=(per_device,...  7.38 us
    split x1, local copies, waits for them, and re-layouts, packed(): return jnp.concatenate(jnp.split(value, count, axis=2), axis=3)  4.97 us
  transfers between devices with their start and end apart: 3, of which 2 were waited for; matrix products, arithmetic and copies ran while one was open for 1% of the time, Pallas kernels for 0%

profile of v1, /device:TPU:0, one launch (start us, length us, event | category | flops | bytes accessed | tf_op | source)
XLA Modules:
  0.0 185.0 jit_solution(1983638274245936665)
XLA Ops:
  7.2 0.0 reduce-scatter.2.cloned.1.call-start
  7.2 5.0 %fusion = (f32[8,2,128,32]{3,2,1,0:T(8,128)S(1)}, f32[8,2,128,32]{3,2,1,0:T(8,128)S(1)}, f32[8,2,128,32]{3,2,1,0:T(8,128)S(1)}, f32[8,2,128,32]{3,2,1,0:T(8,128)...) fusion(f32[8,2,512,128]{3,2,1,0:T(8,128)} %m_ref.3), kind=kLoop, calls=%fused_computation.5 | loop fusion | bytes 4194304 | tf_op jit(solution)/shard_map/split | solution.py:225
  12.2 0.9 pad_maximum_fusion.1
  13.1 1.3 collective-permute-start.1
  14.4 1.9 %pad_maximum_fusion = f32[8,2,128,128]{3,2,1,0:T(8,128)} fusion(f32[8,2,128,32]{3,2,1,0:T(8,128)S(1)} %get-tuple-element.6, f32[8,2,128,32]{3,2,1,0:T(8,128)S(1)} %get-tuple-element.7, f32[8,2,128,32]{3,2,1,0:T(8,128)S(1)} %get-tuple-element.8, f32[8,2,128,32]{3,2,1,0:T(8,128)S(1)} %get-tuple-element.9), kind=kLoop, calls=%fused_computation | loop fusion | flops 786432 | bytes 2097152 | tf_op jit(solution)/shard_map/concatenate | solution.py:225
  16.2 3.1 %collective-permute-start = (f32[8,2,128,128]{3,2,1,0:T(8,128)}, f32[8,2,128,128]{3,2,1,0:T(8,128)S(1)}, u32[]{:S(2)}, u32[]{:S(2)}) collective-permute-start(f32[8,2,128,128]{3,2,1,0:T(8,128)} %pad_maximum_fusion), channel_id=1, source_target_pairs={{0,1},{1,2},{2,3},{3,4},{4,5},{5,6},{6,7},{8,9},{9,10},{10,11},{11... | collective-permute-start | bytes 3145736 | tf_op jit(solution)/shard_map/ppermute | solution.py:235
  19.3 0.5 select_convert_fusion.mask_ref
  19.8 0.0 collective-permute-done.1.right_ref
  19.8 0.0 copy-start
  19.8 1.9 %collective-permute-done.left_ref = f32[8,2,128,128]{3,2,1,0:T(8,128)S(1)} collective-permute-done((f32[8,2,128,128]{3,2,1,0:T(8,128)}, f32[8,2,128,128]{3,2,1,0:T(8,128)S(1)}, u32[]{:S(2)}, u32[]{:S(2)}) %collective-permute-start) | collective-permute-done | bytes 1048608 | tf_op jit(solution)/shard_map/ppermute | solution.py:235
  21.7 0.0 copy-done
  21.7 0.0 copy-start.1
  21.7 1.0 copy-done.1
  22.7 46.6 %stats.1 = f32[8,36,8,128]{3,2,1,0:T(8,128)} custom-call(f32[1,128]{1,0:T(1,128)} %select_convert_fusion.mask_ref, f32[8,2,512,128]{3,2,1,0:T(8,128)} %m_ref.3, f32[8,2,128,128]{3,2,1,0:T(8,128)} %copy-done.1, f32[8,2,128,128]{3,2,1,0:T(8,128)} %copy-done, f32[8,2,512,128]{3,2,1,0:T(8,128)} %rec_ref.3), custom_call_target="tpu_custom_call" | custom-call | tf_op jit(solution)/shard_map/stats/pallas_call | solution.py:243
  69.3 0.0 reduce-scatter.2.cloned.1.call-update
  69.3 58.2 %reduce-scatter.2.cloned.1.call-done = f32[1,36,8,128]{3,2,1,0:T(8,128)} async-done(((f32[8,36,8,128]{3,2,1,0:T(8,128)}), f32[1,36,8,128]{3,2,1,0:T(8,128)}) %reduce-scatter.2.cloned.1.call-update) | async-done | bytes 147472 | tf_op jit(solution)/shard_map/reduce_scatter | solution.py:256
  127.5 18.7 %all-gather = f32[4,36,8,128]{3,2,1,0:T(8,128)} all-gather(f32[1,36,8,128]{3,2,1,0:T(8,128)} %reduce-scatter.2.cloned.1.call-done), channel_id=2, replica_groups=mesh['freq'=4,'trace'=8] {'freq'}, dimensions={0}, use_global_device_ids=true | all-gather | bytes 737280 | tf_op jit(solution)/shard_map/all_gather | solution.py:257
  146.2 7.4 %solve.1 = f32[1,2,32,128]{3,2,1,0:T(8,128)} custom-call(f32[4,1,36,8,128]{4,3,2,1,0:T(8,128)} %bitcast.2), custom_call_target="tpu_custom_call" | custom-call | tf_op jit(solution)/shard_map/solve/pallas_call | solution.py:261
  153.6 0.7 constant_dynamic-slice_fusion
  154.3 10.2 %all_gather.11.h_ref = f32[8,2,8,128]{3,2,1,0:T(8,128)} all-gather(f32[1,2,8,128]{3,2,1,0:T(8,128)S(1)} %constant_dynamic-slice_fusion), channel_id=1, replica_groups=mesh['freq'=4,'trace'=8] {'trace'}, dimensions={0}, use_global_device_ids=true | all-gather | bytes 73728 | tf_op jit(solution)/shard_map/all_gather | solution.py:271
  164.5 0.0 copy-start.2
  164.5 13.0 %forward.1 = f32[8,2,512,128]{3,2,1,0:T(8,128)} custom-call(f32[8,2,8,128]{3,2,1,0:T(8,128)} %all_gather.11.h_ref, f32[8,2,512,128]{3,2,1,0:T(8,128)} %m_ref.3, f32[8,2,128,128]{3,2,1,0:T(8,128)} %copy-done.1, f32[8,2,128,128]{3,2,1,0:T(8,128)} %copy-done, f32[8,2,512,128]{3,2,1,0:T(8,128)} %rec_ref.3), custom_call_target="tpu_custom_call" | custom-call | tf_op jit(solution)/shard_map/forward/pallas_call | solution.py:273
  177.5 0.0 copy-done.2
  177.5 0.6 copy.5
Async XLA Ops:
  7.2 120.4 %reduce-scatter.2.cloned.1.call-start = ((), (), s32[]{:S(2)}) async-start(), calls=%async_computation.1 | async-start | bytes 1327104 | tf_op jit(solution)/shard_map/reduce_scatter | solution.py:256
  13.1 6.8 %collective-permute-start.1 = (f32[8,2,128,128]{3,2,1,0:T(8,128)S(1)}, f32[8,2,128,128]{3,2,1,0:T(8,128)S(1)}, u32[]{:S(2)}, u32[]{:S(2)}) collective-permute-start(f32[8,2,128,128]{3,2,1,0:T(8,128)S(1)} %pad_maximum_fusion.1), channel_id=1, source_target_pairs={{1,0},{2,1},{3,2},{4,3},{5,4},{6,5},{7,6},{9,8},{10,9},{11,10},{12... | collective-permute-start | bytes 3145736 | tf_op jit(solution)/shard_map/ppermute | solution.py:236
  16.2 5.5 %collective-permute-start = (f32[8,2,128,128]{3,2,1,0:T(8,128)}, f32[8,2,128,128]{3,2,1,0:T(8,128)S(1)}, u32[]{:S(2)}, u32[]{:S(2)}) collective-permute-start(f32[8,2,128,128]{3,2,1,0:T(8,128)} %pad_maximum_fusion), channel_id=1, source_target_pairs={{0,1},{1,2},{2,3},{3,4},{4,5},{5,6},{6,7},{8,9},{9,10},{10,11},{11... | collective-permute-start | bytes 3145736 | tf_op jit(solution)/shard_map/ppermute | solution.py:235
  19.8 1.9 %copy-start = (f32[8,2,128,128]{3,2,1,0:T(8,128)}, f32[8,2,128,128]{3,2,1,0:T(8,128)S(1)}, u32[]{:S(2)}) copy-start(f32[8,2,128,128]{3,2,1,0:T(8,128)S(1)} %collective-permute-done.1.right_ref) | copy-start | bytes 3145732
  21.7 1.0 copy-start.1
  164.5 13.0 %copy-start.2 = (f32[8,2,8,128]{3,2,1,0:T(8,128)S(1)}, f32[8,2,8,128]{3,2,1,0:T(8,128)}, u32[]{:S(2)}) copy-start(f32[8,2,8,128]{3,2,1,0:T(8,128)} %all_gather.11.h_ref) | copy-start | bytes 196612
Sparse Core Ops, SparseCore 0:
  69.4 58.0 reduce-scatter.1

commit v2 on v1

--- a/solution.py
+++ b/solution.py
@@ -253,7 +253,8 @@
     extra = per_device * trace_count - shots
     if extra:
         stats = jnp.pad(stats, ((0, extra), (0, 0), (0, 0), (0, 0)))
-    stats = lax.psum_scatter(stats, "trace", scatter_dimension=0, tiled=True)
+    stats = lax.all_to_all(stats, "trace", split_axis=0, concat_axis=0, tiled=True)
+    stats = jnp.sum(stats.reshape((trace_count, per_device) + stats.shape[1:]), axis=0)
     stats = lax.all_gather(stats, "freq", axis=0)
 
     weight = 0.5 * FB * trace_rows * trace_count

time: 186 us -> 152 us (0.82)
  waiting for transfers between devices: 60.1 us -> 18.7 us
  starting transfers between devices: 4.41 us -> 28.2 us
  between operations: 14.1 us -> 0.68 us
  blocking collectives: 28.9 us -> 26.5 us
    reduce_scatter x1 -> x0, waiting for transfers between devices: 58.2 us -> none  [body(): stats = lax.psum_scatter(stats, 'trace', scatter_dimension=0, tiled=True)]
    all_to_all x0 -> x1, starting transfers between devices: none -> 23.8 us  [body(): lax.all_to_all(stats, 'trace', split_axis=0, concat_axis=0, tiled=True)]
    all_to_all x0 -> x1, waiting for transfers between devices: none -> 16.8 us  [body(): lax.all_to_all(stats, 'trace', split_axis=0, concat_axis=0, tiled=True)]
  transfers between devices with their start and end apart: 3 -> 3, of which waited for: 2 -> 2; matrix products, arithmetic and copies ran while one was open for 1% -> 2% of each run, Pallas kernels for 0% -> 0%
where the time goes in v2:
time: 152 us
  Pallas kernels  67 us (44%)
  starting transfers between devices  28.2 us (19%)
  blocking collectives  26.5 us (17%)
  waiting for transfers between devices  18.7 us (12%)
  local copies, waits for them, and re-layouts  7.28 us (5%)
  other arithmetic  3.31 us (2%)
    pallas_call x1, Pallas kernels, body(): pl.pallas_call(stats_kernel, grid=(shots,), in_specs=[pl.BlockSpec((1, LA...  46.6 us
    all_to_all x1, starting transfers between devices, body(): lax.all_to_all(stats, 'trace', split_axis=0, concat_axis=0, tiled=True)  23.8 us
    all_gather x1, blocking collectives, body(): stats = lax.all_gather(stats, 'freq', axis=0)  17.3 us
    all_to_all x1, waiting for transfers between devices, body(): lax.all_to_all(stats, 'trace', split_axis=0, concat_axis=0, tiled=True)  16.8 us
    pallas_call x1, Pallas kernels, body(): pl.pallas_call(forward_kernel, grid=(shots,), in_specs=[pl.BlockSpec((1,...  13 us
    all_gather x1, blocking collectives, body(): taps = lax.all_gather(mine, 'trace', axis=0, tiled=True)[:shots]  9.22 us
    pallas_call x1, Pallas kernels, body(): pl.pallas_call(functools.partial(solve_kernel, weight), grid=(per_device,...  7.39 us
    split x1, local copies, waits for them, and re-layouts, packed(): return jnp.concatenate(jnp.split(value, count, axis=2), axis=3)  4.97 us
  transfers between devices with their start and end apart: 3, of which 2 were waited for; matrix products, arithmetic and copies ran while one was open for 2% of the time, Pallas kernels for 0%

profile of v2, /device:TPU:0, one launch (start us, length us, event | category | flops | bytes accessed | tf_op | source)
XLA Modules:
  0.0 151.7 jit_solution(10081131332256860243)
XLA Ops:
  0.6 5.0 %fusion = (f32[8,2,128,32]{3,2,1,0:T(8,128)S(1)}, f32[8,2,128,32]{3,2,1,0:T(8,128)S(1)}, f32[8,2,128,32]{3,2,1,0:T(8,128)S(1)}, f32[8,2,128,32]{3,2,1,0:T(8,128)...) fusion(f32[8,2,512,128]{3,2,1,0:T(8,128)} %m_ref.3), kind=kLoop, calls=%fused_computation.5 | loop fusion | bytes 4194304 | tf_op jit(solution)/shard_map/split | solution.py:225
  5.6 0.9 pad_maximum_fusion.1
  6.5 1.3 collective-permute-start.1
  7.8 1.9 %pad_maximum_fusion = f32[8,2,128,128]{3,2,1,0:T(8,128)} fusion(f32[8,2,128,32]{3,2,1,0:T(8,128)S(1)} %get-tuple-element.6, f32[8,2,128,32]{3,2,1,0:T(8,128)S(1)} %get-tuple-element.7, f32[8,2,128,32]{3,2,1,0:T(8,128)S(1)} %get-tuple-element.8, f32[8,2,128,32]{3,2,1,0:T(8,128)S(1)} %get-tuple-element.9), kind=kLoop, calls=%fused_computation | loop fusion | flops 786432 | bytes 2097152 | tf_op jit(solution)/shard_map/concatenate | solution.py:225
  9.6 3.1 %collective-permute-start = (f32[8,2,128,128]{3,2,1,0:T(8,128)}, f32[8,2,128,128]{3,2,1,0:T(8,128)S(1)}, u32[]{:S(2)}, u32[]{:S(2)}) collective-permute-start(f32[8,2,128,128]{3,2,1,0:T(8,128)} %pad_maximum_fusion), channel_id=1, source_target_pairs={{0,1},{1,2},{2,3},{3,4},{4,5},{5,6},{6,7},{8,9},{9,10},{10,11},{11... | collective-permute-start | bytes 3145736 | tf_op jit(solution)/shard_map/ppermute | solution.py:235
  12.7 0.5 select_convert_fusion.mask_ref
  13.3 0.0 collective-permute-done.1.right_ref
  13.3 0.0 copy-start
  13.3 1.9 %collective-permute-done.left_ref = f32[8,2,128,128]{3,2,1,0:T(8,128)S(1)} collective-permute-done((f32[8,2,128,128]{3,2,1,0:T(8,128)}, f32[8,2,128,128]{3,2,1,0:T(8,128)S(1)}, u32[]{:S(2)}, u32[]{:S(2)}) %collective-permute-start) | collective-permute-done | bytes 1048608 | tf_op jit(solution)/shard_map/ppermute | solution.py:235
  15.2 0.0 copy-done
  15.2 0.0 copy-start.1
  15.2 1.0 copy-done.1
  16.1 46.6 %stats.1 = f32[8,36,8,128]{3,2,1,0:T(8,128)} custom-call(f32[1,128]{1,0:T(1,128)} %select_convert_fusion.mask_ref, f32[8,2,512,128]{3,2,1,0:T(8,128)} %m_ref.3, f32[8,2,128,128]{3,2,1,0:T(8,128)} %copy-done.1, f32[8,2,128,128]{3,2,1,0:T(8,128)} %copy-done, f32[8,2,512,128]{3,2,1,0:T(8,128)} %rec_ref.3), custom_call_target="tpu_custom_call" | custom-call | tf_op jit(solution)/shard_map/stats/pallas_call | solution.py:243
  62.7 23.8 %all-to-all-start = ((f32[8,36,8,128]{3,2,1,0:T(8,128)}), f32[8,36,8,128]{3,2,1,0:T(8,128)S(1)}, u32[]{:S(2)}, u32[]{:S(2)}) async-start(f32[8,36,8,128]{3,2,1,0:T(8,128)} %stats.1), calls=%async_computation | async-start | bytes 2359296 | tf_op jit(solution)/shard_map/all_to_all | solution.py:256
  86.5 16.8 %all-to-all-done = f32[8,36,8,128]{3,2,1,0:T(8,128)S(1)} async-done(((f32[8,36,8,128]{3,2,1,0:T(8,128)}), f32[8,36,8,128]{3,2,1,0:T(8,128)S(1)}, u32[]{:S(2)}, u32[]{:S(2)}) %all-to-all-start) | async-done | bytes 1179680 | tf_op jit(solution)/shard_map/all_to_all | solution.py:256
  103.3 0.1 reduce_sum.9
  103.4 17.3 %all-gather = f32[144,8,128]{2,1,0:T(8,128)} all-gather(f32[36,8,128]{2,1,0:T(8,128)S(1)} %reduce_sum.9), channel_id=2, replica_groups=mesh['freq'=4,'trace'=8] {'freq'}, dimensions={0}, use_global_device_ids=true | all-gather | bytes 737280 | tf_op jit(solution)/shard_map/all_gather | solution.py:258
  120.7 7.4 %solve.1 = f32[1,2,32,128]{3,2,1,0:T(8,128)} custom-call(f32[4,1,36,8,128]{4,3,2,1,0:T(8,128)} %bitcast.2), custom_call_target="tpu_custom_call" | custom-call | tf_op jit(solution)/shard_map/solve/pallas_call | solution.py:262
  128.1 0.7 constant_dynamic-slice_fusion
  128.8 9.2 %all_gather.11.h_ref = f32[8,2,8,128]{3,2,1,0:T(8,128)} all-gather(f32[1,2,8,128]{3,2,1,0:T(8,128)S(1)} %constant_dynamic-slice_fusion), channel_id=1, replica_groups=mesh['freq'=4,'trace'=8] {'trace'}, dimensions={0}, use_global_device_ids=true | all-gather | bytes 73728 | tf_op jit(solution)/shard_map/all_gather | solution.py:272
  138.0 0.0 copy-start.2
  138.0 13.0 %forward.1 = f32[8,2,512,128]{3,2,1,0:T(8,128)} custom-call(f32[8,2,8,128]{3,2,1,0:T(8,128)} %all_gather.11.h_ref, f32[8,2,512,128]{3,2,1,0:T(8,128)} %m_ref.3, f32[8,2,128,128]{3,2,1,0:T(8,128)} %copy-done.1, f32[8,2,128,128]{3,2,1,0:T(8,128)} %copy-done, f32[8,2,512,128]{3,2,1,0:T(8,128)} %rec_ref.3), custom_call_target="tpu_custom_call" | custom-call | tf_op jit(solution)/shard_map/forward/pallas_call | solution.py:274
  151.0 0.0 copy-done.2
  151.0 0.6 copy.5
Async XLA Ops:
  6.5 6.8 %collective-permute-start.1 = (f32[8,2,128,128]{3,2,1,0:T(8,128)S(1)}, f32[8,2,128,128]{3,2,1,0:T(8,128)S(1)}, u32[]{:S(2)}, u32[]{:S(2)}) collective-permute-start(f32[8,2,128,128]{3,2,1,0:T(8,128)S(1)} %pad_maximum_fusion.1), channel_id=1, source_target_pairs={{1,0},{2,1},{3,2},{4,3},{5,4},{6,5},{7,6},{9,8},{10,9},{11,10},{12... | collective-permute-start | bytes 3145736 | tf_op jit(solution)/shard_map/ppermute | solution.py:236
  9.6 5.5 %collective-permute-start = (f32[8,2,128,128]{3,2,1,0:T(8,128)}, f32[8,2,128,128]{3,2,1,0:T(8,128)S(1)}, u32[]{:S(2)}, u32[]{:S(2)}) collective-permute-start(f32[8,2,128,128]{3,2,1,0:T(8,128)} %pad_maximum_fusion), channel_id=1, source_target_pairs={{0,1},{1,2},{2,3},{3,4},{4,5},{5,6},{6,7},{8,9},{9,10},{10,11},{11... | collective-permute-start | bytes 3145736 | tf_op jit(solution)/shard_map/ppermute | solution.py:235
  13.3 1.9 %copy-start = (f32[8,2,128,128]{3,2,1,0:T(8,128)}, f32[8,2,128,128]{3,2,1,0:T(8,128)S(1)}, u32[]{:S(2)}) copy-start(f32[8,2,128,128]{3,2,1,0:T(8,128)S(1)} %collective-permute-done.1.right_ref) | copy-start | bytes 3145732
  15.2 1.0 copy-start.1
  62.7 40.6 %all-to-all-start = ((f32[8,36,8,128]{3,2,1,0:T(8,128)}), f32[8,36,8,128]{3,2,1,0:T(8,128)S(1)}, u32[]{:S(2)}, u32[]{:S(2)}) async-start(f32[8,36,8,128]{3,2,1,0:T(8,128)} %stats.1), calls=%async_computation | async-start | bytes 2359296 | tf_op jit(solution)/shard_map/all_to_all | solution.py:256
  138.0 13.0 %copy-start.2 = (f32[8,2,8,128]{3,2,1,0:T(8,128)S(1)}, f32[8,2,8,128]{3,2,1,0:T(8,128)}, u32[]{:S(2)}) copy-start(f32[8,2,8,128]{3,2,1,0:T(8,128)} %all_gather.11.h_ref) | copy-start | bytes 196612

commit v3 on v2

--- a/solution.py
+++ b/solution.py
@@ -225,6 +225,11 @@
     return jnp.concatenate(jnp.split(value, count, axis=2), axis=3)
 
 
+def shared(value, axis):
+    copies = jnp.broadcast_to(value, (lax.axis_size(axis),) + value.shape)
+    return lax.all_to_all(copies, axis, split_axis=0, concat_axis=0, tiled=True)
+
+
 def body(recorded, multiples):
     shots, parts, freq_rows, trace_rows = multiples.shape
     blocks = freq_rows // FB
@@ -255,7 +260,7 @@
         stats = jnp.pad(stats, ((0, extra), (0, 0), (0, 0), (0, 0)))
     stats = lax.all_to_all(stats, "trace", split_axis=0, concat_axis=0, tiled=True)
     stats = jnp.sum(stats.reshape((trace_count, per_device) + stats.shape[1:]), axis=0)
-    stats = lax.all_gather(stats, "freq", axis=0)
+    stats = shared(stats, "freq")
 
     weight = 0.5 * FB * trace_rows * trace_count
     all_blocks = blocks * freq_count
@@ -269,7 +274,7 @@
         name="solve",
     )(stats)
     mine = lax.dynamic_slice_in_dim(solved, lax.axis_index("freq") * blocks, blocks, axis=2)
-    taps = lax.all_gather(mine, "trace", axis=0, tiled=True)[:shots]
+    taps = shared(mine, "trace").reshape((-1,) + mine.shape[1:])[:shots]
 
     primaries = pl.pallas_call(
         forward_kernel,

time: 152 us -> 156 us (1.026)
  blocking collectives: 26.5 us -> 48.6 us
  starting transfers between devices: 28.2 us -> 9.26 us
  local copies, waits for them, and re-layouts: 7.28 us -> 8.95 us
    all_to_all x0 -> x2, blocking collectives: none -> 48.6 us  [the longest x1 40.6 us: body(): lax.all_to_all(stats, 'trace', split_axis=0, concat_axis=0, tiled=True)]
    all_gather x2 -> x0, blocking collectives: 26.5 us -> none  [the longest x1 17.3 us: body(): stats = lax.all_gather(stats, 'freq', axis=0)]
    all_to_all x1, starting transfers between devices: 23.8 us -> 4.88 us  [shared(): return lax.all_to_all(copies, axis, split_axis=0, concat_axis=0, tiled=True)]
where the time goes in v3:
time: 156 us; the launch traced here: 155 us
  Pallas kernels  66.9 us (43%)
  blocking collectives  48.6 us (31%)
  waiting for transfers between devices  17.5 us (11%)
  starting transfers between devices  9.26 us (6%)
  local copies, waits for them, and re-layouts  8.95 us (6%)
  other arithmetic  3.31 us (2%)
    pallas_call x1, Pallas kernels, body(): pl.pallas_call(stats_kernel, grid=(shots,), in_specs=[pl.BlockSpec((1, LA...  46.6 us
    all_to_all x1, blocking collectives, body(): lax.all_to_all(stats, 'trace', split_axis=0, concat_axis=0, tiled=True)  40.6 us
    all_to_all x1, waiting for transfers between devices, shared(): return lax.all_to_all(copies, axis, split_axis=0, concat_axis=0, tiled=True)  15.6 us
    pallas_call x1, Pallas kernels, body(): pl.pallas_call(forward_kernel, grid=(shots,), in_specs=[pl.BlockSpec((1,...  13 us
    all_to_all x1, blocking collectives, shared(): return lax.all_to_all(copies, axis, split_axis=0, concat_axis=0, tiled=True)  8.06 us
    pallas_call x1, Pallas kernels, body(): pl.pallas_call(functools.partial(solve_kernel, weight), grid=(per_device,...  7.38 us
    split x1, local copies, waits for them, and re-layouts, packed(): return jnp.concatenate(jnp.split(value, count, axis=2), axis=3)  4.97 us
    all_to_all x1, starting transfers between devices, shared(): return lax.all_to_all(copies, axis, split_axis=0, concat_axis=0, tiled=True)  4.88 us
  transfers between devices with their start and end apart: 3, of which 2 were waited for; matrix products, arithmetic and copies ran while one was open for 2% of the time, Pallas kernels for 0%

profile of v3, /device:TPU:0, one launch (start us, length us, event | category | flops | bytes accessed | tf_op | source)
XLA Modules:
  0.0 155.3 jit_solution(16764443289210576539)
XLA Ops:
  0.6 5.0 %fusion = (f32[8,2,128,32]{3,2,1,0:T(8,128)S(1)}, f32[8,2,128,32]{3,2,1,0:T(8,128)S(1)}, f32[8,2,128,32]{3,2,1,0:T(8,128)S(1)}, f32[8,2,128,32]{3,2,1,0:T(8,128)...) fusion(f32[8,2,512,128]{3,2,1,0:T(8,128)} %m_ref.3), kind=kLoop, calls=%fused_computation.5 | loop fusion | bytes 4194304 | tf_op jit(solution)/shard_map/split | solution.py:225
  5.6 0.9 pad_maximum_fusion.1
  6.5 1.3 collective-permute-start.1
  7.8 1.9 %pad_maximum_fusion = f32[8,2,128,128]{3,2,1,0:T(8,128)} fusion(f32[8,2,128,32]{3,2,1,0:T(8,128)S(1)} %get-tuple-element.6, f32[8,2,128,32]{3,2,1,0:T(8,128)S(1)} %get-tuple-element.7, f32[8,2,128,32]{3,2,1,0:T(8,128)S(1)} %get-tuple-element.8, f32[8,2,128,32]{3,2,1,0:T(8,128)S(1)} %get-tuple-element.9), kind=kLoop, calls=%fused_computation | loop fusion | flops 786432 | bytes 2097152 | tf_op jit(solution)/shard_map/concatenate | solution.py:225
  9.6 3.1 %collective-permute-start = (f32[8,2,128,128]{3,2,1,0:T(8,128)}, f32[8,2,128,128]{3,2,1,0:T(8,128)S(1)}, u32[]{:S(2)}, u32[]{:S(2)}) collective-permute-start(f32[8,2,128,128]{3,2,1,0:T(8,128)} %pad_maximum_fusion), channel_id=1, source_target_pairs={{0,1},{1,2},{2,3},{3,4},{4,5},{5,6},{6,7},{8,9},{9,10},{10,11},{11... | collective-permute-start | bytes 3145736 | tf_op jit(solution)/shard_map/ppermute | solution.py:240
  12.7 0.5 select_convert_fusion.mask_ref
  13.3 0.0 collective-permute-done.1.right_ref
  13.3 0.0 copy-start
  13.3 1.9 %collective-permute-done.left_ref = f32[8,2,128,128]{3,2,1,0:T(8,128)S(1)} collective-permute-done((f32[8,2,128,128]{3,2,1,0:T(8,128)}, f32[8,2,128,128]{3,2,1,0:T(8,128)S(1)}, u32[]{:S(2)}, u32[]{:S(2)}) %collective-permute-start) | collective-permute-done | bytes 1048608 | tf_op jit(solution)/shard_map/ppermute | solution.py:240
  15.2 0.0 copy-done
  15.2 0.0 copy-start.1
  15.2 1.0 copy-done.1
  16.1 46.6 %stats.1 = f32[8,36,8,128]{3,2,1,0:T(8,128)} custom-call(f32[1,128]{1,0:T(1,128)} %select_convert_fusion.mask_ref, f32[8,2,512,128]{3,2,1,0:T(8,128)} %m_ref.3, f32[8,2,128,128]{3,2,1,0:T(8,128)} %copy-done.1, f32[8,2,128,128]{3,2,1,0:T(8,128)} %copy-done, f32[8,2,512,128]{3,2,1,0:T(8,128)} %rec_ref.3), custom_call_target="tpu_custom_call" | custom-call | tf_op jit(solution)/shard_map/stats/pallas_call | solution.py:248
  62.7 40.6 %all_to_all.15 = f32[8,36,8,128]{3,2,1,0:T(8,128)S(1)} all-to-all(f32[8,36,8,128]{3,2,1,0:T(8,128)} %stats.1), channel_id=1, replica_groups=mesh['freq'=4,'trace'=8] {'trace'}, dimensions={0} | all-to-all | bytes 2359296 | tf_op jit(solution)/shard_map/all_to_all | solution.py:261
  103.3 0.1 reduce_sum.9
  103.3 0.9 broadcast_in_dim.17
  104.2 4.9 %all-to-all-start.1 = ((f32[4,1,36,8,128]{4,3,2,1,0:T(8,128)}), f32[4,1,36,8,128]{4,3,2,1,0:T(8,128)S(1)}, u32[]{:S(2)}, u32[]{:S(2)}) async-start(f32[4,1,36,8,128]{4,3,2,1,0:T(8,128)} %broadcast_in_dim.17), calls=%async_computation.1 | async-start | bytes 1179648 | tf_op jit(solution)/shard_map/all_to_all | solution.py:230
  109.1 15.6 %all-to-all-done.1.st_ref = f32[4,1,36,8,128]{4,3,2,1,0:T(8,128)S(1)} async-done(((f32[4,1,36,8,128]{4,3,2,1,0:T(8,128)}), f32[4,1,36,8,128]{4,3,2,1,0:T(8,128)S(1)}, u32[]{:S(2)}, u32[]{:S(2)}) %all-to-all-start.1) | async-done | bytes 589856 | tf_op jit(solution)/shard_map/all_to_all | solution.py:230
  124.7 0.0 copy-start.2
  124.7 0.8 copy-done.2
  125.5 7.4 %solve.1 = f32[1,2,32,128]{3,2,1,0:T(8,128)} custom-call(f32[4,1,36,8,128]{4,3,2,1,0:T(8,128)} %copy-done.2), custom_call_target="tpu_custom_call" | custom-call | tf_op jit(solution)/shard_map/solve/pallas_call | solution.py:267
  132.9 0.7 dynamic-slice_bitcast_fusion
  133.6 8.1 %all_to_all.16 = f32[8,1,2,8,128]{4,3,2,1,0:T(8,128)} all-to-all(f32[8,1,2,8,128]{4,3,2,1,0:T(8,128)S(1)} %broadcast_in_dim.18), channel_id=1, replica_groups=mesh['freq'=4,'trace'=8] {'trace'}, dimensions={0} | all-to-all | bytes 131072 | tf_op jit(solution)/shard_map/all_to_all | solution.py:230
  141.6 0.0 copy-start.3
  141.6 13.0 %forward.1 = f32[8,2,512,128]{3,2,1,0:T(8,128)} custom-call(f32[8,2,8,128]{3,2,1,0:T(8,128)} %bitcast.4, f32[8,2,512,128]{3,2,1,0:T(8,128)} %m_ref.3, f32[8,2,128,128]{3,2,1,0:T(8,128)} %copy-done.1, f32[8,2,128,128]{3,2,1,0:T(8,128)} %copy-done, f32[8,2,512,128]{3,2,1,0:T(8,128)} %rec_ref.3), custom_call_target="tpu_custom_call" | custom-call | tf_op jit(solution)/shard_map/forward/pallas_call | solution.py:279
  154.6 0.0 copy-done.3
  154.6 0.6 copy.5
  (1 shorter events, 0.0 us)
Async XLA Ops:
  6.5 6.8 %collective-permute-start.1 = (f32[8,2,128,128]{3,2,1,0:T(8,128)S(1)}, f32[8,2,128,128]{3,2,1,0:T(8,128)S(1)}, u32[]{:S(2)}, u32[]{:S(2)}) collective-permute-start(f32[8,2,128,128]{3,2,1,0:T(8,128)S(1)} %pad_maximum_fusion.1), channel_id=1, source_target_pairs={{1,0},{2,1},{3,2},{4,3},{5,4},{6,5},{7,6},{9,8},{10,9},{11,10},{12... | collective-permute-start | bytes 3145736 | tf_op jit(solution)/shard_map/ppermute | solution.py:241
  9.6 5.5 %collective-permute-start = (f32[8,2,128,128]{3,2,1,0:T(8,128)}, f32[8,2,128,128]{3,2,1,0:T(8,128)S(1)}, u32[]{:S(2)}, u32[]{:S(2)}) collective-permute-start(f32[8,2,128,128]{3,2,1,0:T(8,128)} %pad_maximum_fusion), channel_id=1, source_target_pairs={{0,1},{1,2},{2,3},{3,4},{4,5},{5,6},{6,7},{8,9},{9,10},{10,11},{11... | collective-permute-start | bytes 3145736 | tf_op jit(solution)/shard_map/ppermute | solution.py:240
  13.3 1.9 %copy-start = (f32[8,2,128,128]{3,2,1,0:T(8,128)}, f32[8,2,128,128]{3,2,1,0:T(8,128)S(1)}, u32[]{:S(2)}) copy-start(f32[8,2,128,128]{3,2,1,0:T(8,128)S(1)} %collective-permute-done.1.right_ref) | copy-start | bytes 3145732
  15.2 1.0 copy-start.1
  104.2 20.5 %all-to-all-start.1 = ((f32[4,1,36,8,128]{4,3,2,1,0:T(8,128)}), f32[4,1,36,8,128]{4,3,2,1,0:T(8,128)S(1)}, u32[]{:S(2)}, u32[]{:S(2)}) async-start(f32[4,1,36,8,128]{4,3,2,1,0:T(8,128)} %broadcast_in_dim.17), calls=%async_computation.1 | async-start | bytes 1179648 | tf_op jit(solution)/shard_map/all_to_all | solution.py:230
  124.7 0.8 copy-start.2
  141.6 13.0 %copy-start.3 = (f32[8,1,2,8,128]{4,3,2,1,0:T(8,128)S(1)}, f32[8,1,2,8,128]{4,3,2,1,0:T(8,128)}, u32[]{:S(2)}) copy-start(f32[8,1,2,8,128]{4,3,2,1,0:T(8,128)} %all_to_all.16) | copy-start | bytes 196612
